TPU v7x, 32 devices: a whole 2x2x4 slice. The times are simulated.
32 devices in a mesh: emb: 8 (over z, core), dp: 4 (over y, x).
Axes of the slice: x: 2, y: 2, z: 4, core: 2. Of those that a mesh axis runs over, the one named last changes fastest.
Arguments:
- embeddings: bfloat16 [512, 256, 256], P('emb', 'dp'), may hold values from -9 to 9
- machine_projection: bfloat16 [512, 32], replicated, may hold values from -0.015625 to 0.015625
- w_lcb: bfloat16 [512, 512], P('dp'), may hold values from -0.25 to 0.25
- w_fmb: bfloat16 [32, 256], replicated, may hold values from -1 to 1
- ln_gain: float32 [512, 256], P('emb'), may hold values from 0.5 to 1.5
- ln_bias: float32 [512, 256], P('emb'), may hold values from -1.8 to 1.8
Outputs:
- layer_out: bfloat16 [512, 256, 256], P('emb', 'dp')
All inputs are finite; a program needn't handle non-finite values.
Results may differ from a plain program's by a relative error of at most 0.007.
Values may be sent and summed in bfloat16 or wider, within the bound.
A program may use at most 64 MiB of HBM per device.

v0:
```python
import functools

import jax
import jax.numpy as jnp
from jax import lax
from jax.experimental import pallas as pl
from jax.experimental.pallas import tpu as pltpu
from jax.sharding import PartitionSpec as P

MESH = pl.DeviceIdType.MESH
LANES = 128
VMEM_LIMIT = 40 * 1024 * 1024


def sample_kernel(
    emb_size, dp_size, group, eps,
    x_ref, w_ref, proj_ref, fmb_ref, y_ref,
    got, done, mixed_ref, weights,
    w_send, w_recv, in_send, in_recv, out_send, out_recv, local_sem,
):
    me = lax.axis_index("emb")
    mine = lax.axis_index("dp")
    share = got.shape[0]
    rows = x_ref.shape[1]
    w_rows = w_ref.shape[0]
    entries = float(got.shape[1] * got.shape[2])
    emb_offsets = list(range(1, emb_size))
    dp_offsets = list(range(1, dp_size))

    barrier = pltpu.get_barrier_semaphore()
    for k in emb_offsets:
        pl.semaphore_signal(
            barrier, inc=1, device_id={"emb": lax.rem(me + k, emb_size)}, device_id_type=MESH
        )
    for k in dp_offsets:
        pl.semaphore_signal(
            barrier, inc=1, device_id={"dp": lax.rem(mine + k, dp_size)}, device_id_type=MESH
        )
    pl.semaphore_wait(barrier, len(emb_offsets) + len(dp_offsets))

    def w_copy(k):
        return pltpu.make_async_remote_copy(
            src_ref=w_ref,
            dst_ref=weights.at[pl.ds(pl.multiple_of(mine * w_rows, w_rows), w_rows)],
            send_sem=w_send.at[k],
            recv_sem=w_recv.at[k],
            device_id={"dp": lax.rem(mine + k, dp_size)},
            device_id_type=MESH,
        )

    def in_copy(c, k):
        peer = lax.rem(me + k, emb_size)
        return pltpu.make_async_remote_copy(
            src_ref=x_ref.at[pl.ds(peer * share + c * group, group)],
            dst_ref=got.at[pl.ds(c * group, group), pl.ds(pl.multiple_of(me * rows, rows), rows)],
            send_sem=in_send.at[c, k],
            recv_sem=in_recv.at[c, k],
            device_id={"emb": peer},
            device_id_type=MESH,
        )

    def out_copy(c, k):
        peer = lax.rem(me + k, emb_size)
        return pltpu.make_async_remote_copy(
            src_ref=done.at[pl.ds(c * group, group), pl.ds(pl.multiple_of(peer * rows, rows), rows)],
            dst_ref=y_ref.at[pl.ds(me * share + c * group, group)],
            send_sem=out_send.at[c, k],
            recv_sem=out_recv.at[c, k],
            device_id={"emb": peer},
            device_id_type=MESH,
        )

    def own_in(c):
        return pltpu.make_async_copy(
            x_ref.at[pl.ds(me * share + c * group, group)],
            got.at[pl.ds(c * group, group), pl.ds(pl.multiple_of(me * rows, rows), rows)],
            in_recv.at[c, 0],
        )

    def own_out(c):
        return pltpu.make_async_copy(
            done.at[pl.ds(c * group, group), pl.ds(pl.multiple_of(me * rows, rows), rows)],
            y_ref.at[pl.ds(me * share + c * group, group)],
            out_recv.at[c, 0],
        )

    own_w = pltpu.make_async_copy(
        w_ref, weights.at[pl.ds(pl.multiple_of(mine * w_rows, w_rows), w_rows)], local_sem
    )
    own_w.start()
    for k in dp_offsets:
        w_copy(k).start()

    @pl.loop(0, share // group)
    def _(c):
        for k in emb_offsets:
            in_copy(c, k).start()
        own_in(c).start()

    own_w.wait()
    for k in dp_offsets:
        w_copy(k).wait()

    @pl.loop(0, share // group)
    def _(c):
        own_in(c).wait()
        for k in emb_offsets:
            in_copy(c, k).wait_recv()

        @pl.loop(c * group, (c + 1) * group)
        def _(b):
            x = got[b]
            factor = jnp.dot(proj_ref[...], x, preferred_element_type=jnp.float32).astype(jnp.bfloat16)
            inner = lax.dot_general(
                x, factor, (((1,), (1,)), ((), ())), preferred_element_type=jnp.float32
            ).astype(jnp.bfloat16)
            mixed_ref[...] = (
                jnp.dot(weights[...], x, preferred_element_type=jnp.float32)
                + jnp.dot(inner, fmb_ref[...], preferred_element_type=jnp.float32)
                + x.astype(jnp.float32)
            )
            mixed = mixed_ref[...]
            average = jnp.sum(mixed) / entries
            centered = mixed - average
            spread = jnp.sum(centered * centered) / entries
            scale = lax.rsqrt(jnp.full((1, x.shape[1]), spread + eps, jnp.float32))
            done[b] = (centered * scale).astype(jnp.bfloat16)

        for k in emb_offsets:
            out_copy(c, k).start()
        own_out(c).start()

    @pl.loop(0, share // group)
    def _(c):
        own_out(c).wait()
        for k in emb_offsets:
            in_copy(c, k).wait_send()
            out_copy(c, k).wait()


def sample_body(embeddings, machine_projection, w_lcb, w_fmb, ln_gain, ln_bias):
    emb_size = lax.axis_size("emb")
    dp_size = lax.axis_size("dp")
    rows, samples, width = embeddings.shape
    share = samples // emb_size
    emb_count = w_lcb.shape[1]
    group = 4 if share % 8 == 0 else 2 if share % 2 == 0 else 1
    x = embeddings.transpose(1, 0, 2)
    vmem = pl.BlockSpec(memory_space=pltpu.VMEM)
    y = pl.pallas_call(
        functools.partial(sample_kernel, emb_size, dp_size, group, 1e-05),
        out_shape=jax.ShapeDtypeStruct((samples, rows, width), jnp.bfloat16),
        in_specs=[vmem] * 4,
        out_specs=vmem,
        scratch_shapes=[
            pltpu.VMEM((share, emb_count, width), jnp.bfloat16),
            pltpu.VMEM((share, emb_count, width), jnp.bfloat16),
            pltpu.VMEM((emb_count, width), jnp.float32),
            pltpu.VMEM((emb_count, emb_count), jnp.bfloat16),
            pltpu.SemaphoreType.DMA((dp_size,)),
            pltpu.SemaphoreType.DMA((dp_size,)),
            pltpu.SemaphoreType.DMA((share // group, emb_size)),
            pltpu.SemaphoreType.DMA((share // group, emb_size)),
            pltpu.SemaphoreType.DMA((share // group, emb_size)),
            pltpu.SemaphoreType.DMA((share // group, emb_size)),
            pltpu.SemaphoreType.DMA(()),
        ],
        compiler_params=pltpu.CompilerParams(
            collective_id=0, has_side_effects=True, vmem_limit_bytes=40 * 1024 * 1024
        ),
    )(x, w_lcb, machine_projection.T, w_fmb)
    scaled = y.transpose(1, 0, 2).astype(jnp.float32)
    return (scaled * ln_gain[:, None, :] + ln_bias[:, None, :]).astype(jnp.bfloat16)


def tile_kernel(
    emb_size, dp_size, cores, eps,
    x_hbm, w_hbm, proj_hbm, fmb_hbm, gain_hbm, bias_hbm, y_ref,
    own, got, done, back, wide, spaced, mixed_ref, weights, factors, affine,
    w_send, w_recv, send_sem, in_recv, out_recv, load_sem, outer, beside, far,
):
    me = lax.axis_index("emb")
    mine = lax.axis_index("dp")
    chips = emb_size // cores
    chip = me // cores
    emb_count, share, width = got.shape
    rows = x_hbm.shape[0]
    w_rows = w_hbm.shape[0]
    block = rows * share
    others = emb_size - 1
    entries = float(emb_count * width)
    columns = [pl.ds(c, LANES) for c in range(0, width, LANES)]
    near = [sign * step for step in range(1, chips) for sign in (1, -1)]
    half = max(chips // 2, 1)
    dp_bits = [1 << i for i in range(dp_size.bit_length() - 1)]

    def inside(other):
        return (other >= 0) & (other < chips)

    def on_chip(step, action):
        other = chip + step

        @pl.when(inside(other))
        def _():
            for k in range(cores):
                peer = other * cores + k
                if step:
                    action(peer)
                else:
                    pl.when(peer != me)(functools.partial(action, peer))

    def same_side_then_across(action):
        for crossing in (False, True):
            for step in reversed(near) if crossing else near:
                other = chip + step
                across = (other // half) != (chip // half)

                @pl.when(inside(other) & (across if crossing else jnp.logical_not(across)))
                def _():
                    for k in range(cores):
                        action(other * cores + k)
            if not crossing:
                on_chip(0, action)

    def dp_partner(bit):
        return mine + bit * (1 - 2 * lax.rem(mine // bit, 2))

    def of_peer(ref, peer):
        return ref.at[:, pl.ds(pl.multiple_of(peer * share, share), share)]

    def signal(semaphore, peer):
        pl.semaphore_signal(semaphore, inc=1, device_id={"emb": peer}, device_id_type=MESH)

    inward = 1 - 2 * (chip // half if chips > 1 else chip)
    inward = jnp.maximum(inward, -1)
    middle = (chip == half - 1) | (chip == half)
    core = lax.rem(me, cores)
    neighbours = (me + inward * cores, me - inward * cores)
    there = (inside(chip + inward), inside(chip - inward))

    barrier = pltpu.get_barrier_semaphore()
    pl.when(there[0] & middle)(functools.partial(signal, barrier, neighbours[0]))
    pl.when(there[1])(functools.partial(signal, barrier, neighbours[1]))

    @pl.when(core == 0)
    def _():
        for bit in dp_bits:
            pl.semaphore_signal(barrier, inc=1, device_id={"dp": dp_partner(bit)}, device_id_type=MESH)

    @pl.when(core != 0)
    def _():
        signal(barrier, me - core)

    own_in = pltpu.make_async_copy(of_peer(x_hbm, me), own, load_sem.at[0])
    own_w = pltpu.make_async_copy(
        w_hbm, weights.at[pl.ds(pl.multiple_of(mine * w_rows, w_rows), w_rows)], load_sem.at[1]
    )

    def in_copy(source, peer):
        return pltpu.make_async_remote_copy(
            src_ref=of_peer(x_hbm, peer),
            dst_ref=got.at[pl.ds(source * rows, rows)],
            send_sem=send_sem,
            recv_sem=in_recv,
            device_id={"emb": peer},
            device_id_type=MESH,
        )

    def last_source(receiver):
        return jnp.where(receiver // cores < half, half, half - 1) * cores + cores - 1

    def out_copy(source, peer):
        return pltpu.make_async_remote_copy(
            src_ref=done.at[pl.ds(peer * rows, rows)],
            dst_ref=back.at[source],
            send_sem=send_sem,
            recv_sem=out_recv.at[(source == last_source(peer)).astype(jnp.int32)],
            device_id={"emb": peer},
            device_id_type=MESH,
        )

    def w_copy(i):
        bit = dp_bits[i]
        held = pl.multiple_of((mine // bit) * (bit * w_rows), bit * w_rows)
        part = weights.at[pl.ds(held, bit * w_rows)]
        return pltpu.make_async_remote_copy(
            src_ref=part,
            dst_ref=part,
            send_sem=w_send,
            recv_sem=w_recv.at[i],
            device_id={"dp": dp_partner(bit)},
            device_id_type=MESH,
        )

    def w_pass(peer):
        return pltpu.make_async_remote_copy(
            src_ref=weights,
            dst_ref=weights,
            send_sem=w_send,
            recv_sem=w_recv.at[0],
            device_id={"emb": peer},
            device_id_type=MESH,
        )

    def wait_for(ref, semaphore):
        pltpu.make_async_copy(ref, ref, semaphore).wait()

    def tell(distance):
        for sign in (1, -1):
            @pl.when(inside(chip + sign * (distance - 1)) & inside(chip - sign))
            def _():
                signal(far.at[distance - 2], me - sign * cores)

    def heard(distance):
        count = inside(chip + distance).astype(jnp.int32) + inside(chip - distance).astype(jnp.int32)

        @pl.when(count > 0)
        def _():
            pl.semaphore_wait(far.at[distance - 2], count)

    pl.semaphore_wait(
        barrier,
        there[0].astype(jnp.int32) + jnp.where(core == 0, cores - 1 + len(dp_bits), 0),
    )
    pl.when(there[0])(lambda: in_copy(me, neighbours[0]).start())
    own_in.start()
    pl.when(there[0] & jnp.logical_not(middle))(functools.partial(signal, outer, neighbours[0]))

    @pl.when(there[1])
    def _():
        pl.semaphore_wait(outer, 1)
        in_copy(me, neighbours[1]).start()

    @pl.when(core == 0)
    def _():
        own_w.start()
        for k in range(1, cores):
            signal(beside, me + k)
        if cores > 1:
            pl.semaphore_wait(beside, cores - 1)

    @pl.when(core != 0)
    def _():
        pl.semaphore_wait(beside, 1)
        signal(beside, me - core)

    for source, target in ((proj_hbm, factors.at[:, pl.ds(0, emb_count)]), (fmb_hbm, factors.at[:, pl.ds(emb_count, width)])):
        pltpu.make_async_copy(source, target, load_sem.at[2]).start()
    for i, source in enumerate((gain_hbm, bias_hbm)):
        pltpu.make_async_copy(source, affine.at[i], load_sem.at[3]).start()
    if chips > 2:
        tell(2)

    for k in range(cores):
        for distance in range(chips):
            if k == 0 and distance >= 2:
                heard(distance)
                if distance < chips - 1:
                    tell(distance + 1)
            for step in (distance, -distance) if distance else (0,):
                peer = (chip + step) * cores + k
                left = peer != me + step * cores if distance < 2 else True

                @pl.when(inside(chip + step) & left)
                def _():
                    in_copy(me, peer).start()

    @pl.when(core == 0)
    def _():
        own_w.wait()
        for i in range(len(dp_bits)):
            w_copy(i).start()
            w_copy(i).wait_recv()
        for k in range(1, cores):
            w_pass(me + k).start()

    @pl.when(core != 0)
    def _():
        w_pass(me - core).wait_recv()

    wait_for(factors, load_sem.at[2])
    wait_for(affine, load_sem.at[3])

    def widen(source, taken):
        taken = taken.astype(jnp.float32).reshape(block, width)
        for c in range(len(columns)):
            wide[c, pl.ds(pl.multiple_of(source * block, block), block)] = taken[:, c * LANES:(c + 1) * LANES]

    own_in.wait()
    widen(me, own[...])
    wait_for(got.at[pl.ds(0, others * rows)], in_recv)

    @pl.loop(0, emb_size)
    def _(source):
        @pl.when(source != me)
        def _():
            widen(source, got[pl.ds(source * rows, rows)])

    @pl.loop(0, share)
    def _(b):
        x = jnp.concatenate(
            [wide[c, pl.ds(b, emb_count, stride=share), :] for c in range(len(columns))], axis=1
        ).astype(jnp.bfloat16)
        factor = jnp.dot(
            factors[:, :emb_count], x, preferred_element_type=jnp.float32
        ).astype(jnp.bfloat16)
        inner = lax.dot_general(
            x, factor, (((1,), (1,)), ((), ())), preferred_element_type=jnp.float32
        ).astype(jnp.bfloat16)
        mixed_ref[...] = (
            jnp.dot(weights[...], x, preferred_element_type=jnp.float32)
            + jnp.dot(inner, factors[:, emb_count:], preferred_element_type=jnp.float32)
            + x.astype(jnp.float32)
        )
        mixed = mixed_ref[...]
        average = jnp.sum(mixed) / entries
        centered = mixed - average
        spread = jnp.sum(centered * centered) / entries
        scale = lax.rsqrt(jnp.full((1, width), spread + eps, jnp.float32))
        scaled = centered * scale
        for c in range(len(columns)):
            spaced[c, pl.ds(b, emb_count, stride=share), :] = scaled[:, c * LANES:(c + 1) * LANES]

    def narrow(target):
        for c, column in enumerate(columns):
            done[pl.ds(target * rows, rows), :, column] = (
                spaced[c, pl.ds(pl.multiple_of(target * block, block), block)]
                .reshape(rows, share, LANES)
                .astype(jnp.bfloat16)
            )

    def land(source, taken):
        y_ref[:, pl.ds(pl.multiple_of(source * share, share), share), :] = (
            taken.astype(jnp.float32) * affine[0][:, None, :] + affine[1][:, None, :]
        ).astype(jnp.bfloat16)

    pl.loop(0, emb_size)(narrow)
    land(me, done[pl.ds(me * rows, rows)])
    same_side_then_across(lambda peer: out_copy(me, peer).start())

    @pl.when(core == 0)
    def _():
        wait_for(weights.at[pl.ds(0, (dp_size - 1) * w_rows)], w_send)
        for k in range(1, cores):
            w_pass(me + k).wait_send()


    last = last_source(me)
    wait_for(back.at[pl.ds(0, others - 1)], out_recv.at[0])

    @pl.loop(0, emb_size)
    def _(source):
        @pl.when((source != me) & (source != last))
        def _():
            land(source, back[source])

    wait_for(back.at[0], out_recv.at[1])
    land(last, back[last])
    wait_for(wide.at[:, pl.ds(0, others * block)], send_sem)


def write_kernel(y_ref, out_ref, sem):
    copy = pltpu.make_async_copy(y_ref, out_ref, sem)
    copy.start()
    copy.wait()


def tile_body(embeddings, machine_projection, w_lcb, w_fmb, ln_gain, ln_bias):
    emb_size = lax.axis_size("emb")
    dp_size = lax.axis_size("dp")
    rows, samples, width = embeddings.shape
    share = samples // emb_size
    emb_count, rank = machine_projection.shape
    cores = 2 if emb_size % 2 == 0 else 1
    dma = pltpu.SemaphoreType.DMA
    y = pl.pallas_call(
        functools.partial(tile_kernel, emb_size, dp_size, cores, 1e-05),
        out_shape=pltpu.VMEM((rows, samples, width), jnp.bfloat16),
        in_specs=[pl.BlockSpec(memory_space=pltpu.HBM)] * 6,
        out_specs=pl.BlockSpec(memory_space=pltpu.VMEM),
        scratch_shapes=[
            pltpu.VMEM((rows, share, width), jnp.bfloat16),
            pltpu.VMEM((emb_count, share, width), jnp.bfloat16),
            pltpu.VMEM((emb_count, share, width), jnp.bfloat16),
            pltpu.VMEM((emb_size, rows, share, width), jnp.bfloat16),
            pltpu.VMEM((width // LANES, emb_count * share, LANES), jnp.float32),
            pltpu.VMEM((width // LANES, emb_count * share, LANES), jnp.float32),
            pltpu.VMEM((emb_count, width), jnp.float32),
            pltpu.VMEM((emb_count, emb_count), jnp.bfloat16),
            pltpu.VMEM((rank, emb_count + width), jnp.bfloat16),
            pltpu.VMEM((2, rows, width), jnp.float32),
            dma(()),
            dma((dp_size.bit_length() - 1,)),
            dma(()),
            dma(()),
            dma((2,)),
            dma((4,)),
            pltpu.SemaphoreType.REGULAR,
            pltpu.SemaphoreType.REGULAR,
            pltpu.SemaphoreType.REGULAR((max(emb_size // cores - 2, 1),)),
        ],
        compiler_params=pltpu.CompilerParams(
            collective_id=0, has_side_effects=True, vmem_limit_bytes=VMEM_LIMIT
        ),
    )(
        *(
            pltpu.with_memory_space_constraint(array, pltpu.HBM)
            for array in (embeddings, w_lcb, machine_projection.T, w_fmb, ln_gain, ln_bias)
        )
    )
    return pl.pallas_call(
        write_kernel,
        out_shape=jax.ShapeDtypeStruct(y.shape, y.dtype),
        in_specs=[pl.BlockSpec(memory_space=pltpu.VMEM)],
        out_specs=pl.BlockSpec(memory_space=pltpu.HBM),
        scratch_shapes=[dma(())],
        compiler_params=pltpu.CompilerParams(vmem_limit_bytes=4 * 1024 * 1024),
    )(y)


def body(embeddings, *rest):
    share = embeddings.shape[1] // lax.axis_size("emb")
    dp_size = lax.axis_size("dp")
    whole_tiles = share % 8 == 0 and lax.axis_size("emb") % 4 == 0 and dp_size > 1 and dp_size & (dp_size - 1) == 0
    return (tile_body if whole_tiles else sample_body)(embeddings, *rest)


def solution(mesh):
    return jax.shard_map(
        body,
        mesh=mesh,
        in_specs=(P("emb", "dp", None), P(), P("dp", None), P(), P("emb", None), P("emb", None)),
        out_specs=P("emb", "dp", None),
        check_vma=False,
    )
```

profile of v0, /device:TPU:9, one launch (start us, length us, event | category | flops | bytes accessed | tf_op | source)
XLA Modules:
  0.0 94.2 jit_solution(4616510778455279427)
XLA Ops:
  0.0 92.9 %shard_map.64.y_ref = bf16[64,64,256]{2,1,0:T(8,128)(2,1)S(1)} custom-call(bf16[64,64,256]{2,1,0:T(8,128)(2,1)} %x_hbm.1, bf16[128,512]{1,0:T(8,128)(2,1)} %w_hbm.1, bf16[32,512]{1,0:T(8,128)(2,1)} %bitcast.1, bf16[32,256]{1,0:T(8,128)(2,1)} %fmb_hbm.1, f32[64,256]{1,0:T(8,128)} %gain_hbm.1, f32[64,256]{1,0:T(8,128)} %bias_hbm.1), custom_call_target="tpu_custom_call" | custom-call | tf_op jit(solution)/shard_map/pallas_call | solution.py:476
  92.9 1.3 %shard_map.65 = bf16[64,64,256]{2,1,0:T(8,128)(2,1)} custom-call(bf16[64,64,256]{2,1,0:T(8,128)(2,1)S(1)} %shard_map.64.y_ref), custom_call_target="tpu_custom_call" | custom-call | tf_op jit(solution)/shard_map/pallas_call | solution.py:511
where the time goes:
time: 94.3 us; the launch traced here: 94.2 us
  Pallas kernels  94.2 us (100%)
    pallas_call x1, Pallas kernels, tile_body(): pl.pallas_call(functools.partial(tile_kernel, emb_size, dp_size, cores, 1...  92.9 us

commit v1 on v0

--- a/solution.py
+++ b/solution.py
@@ -344,7 +344,8 @@
         pl.semaphore_wait(beside, 1)
         signal(beside, me - core)
 
-    for source, target in ((proj_hbm, factors.at[:, pl.ds(0, emb_count)]), (fmb_hbm, factors.at[:, pl.ds(emb_count, width)])):
+    for source, first in ((proj_hbm, 0), (fmb_hbm, emb_count)):
+        target = factors.at[:, pl.ds(first, source.shape[1])]
         pltpu.make_async_copy(source, target, load_sem.at[2]).start()
     for i, source in enumerate((gain_hbm, bias_hbm)):
         pltpu.make_async_copy(source, affine.at[i], load_sem.at[3]).start()
@@ -444,7 +445,6 @@
         for k in range(1, cores):
             w_pass(me + k).wait_send()
 
-
     last = last_source(me)
     wait_for(back.at[pl.ds(0, others - 1)], out_recv.at[0])
 
@@ -457,12 +457,6 @@
     wait_for(back.at[0], out_recv.at[1])
     land(last, back[last])
     wait_for(wide.at[:, pl.ds(0, others * block)], send_sem)
-
-
-def write_kernel(y_ref, out_ref, sem):
-    copy = pltpu.make_async_copy(y_ref, out_ref, sem)
-    copy.start()
-    copy.wait()
 
 
 def tile_body(embeddings, machine_projection, w_lcb, w_fmb, ln_gain, ln_bias):
@@ -473,7 +467,7 @@
     emb_count, rank = machine_projection.shape
     cores = 2 if emb_size % 2 == 0 else 1
     dma = pltpu.SemaphoreType.DMA
-    y = pl.pallas_call(
+    return pl.pallas_call(
         functools.partial(tile_kernel, emb_size, dp_size, cores, 1e-05),
         out_shape=pltpu.VMEM((rows, samples, width), jnp.bfloat16),
         in_specs=[pl.BlockSpec(memory_space=pltpu.HBM)] * 6,
@@ -508,14 +502,6 @@
             for array in (embeddings, w_lcb, machine_projection.T, w_fmb, ln_gain, ln_bias)
         )
     )
-    return pl.pallas_call(
-        write_kernel,
-        out_shape=jax.ShapeDtypeStruct(y.shape, y.dtype),
-        in_specs=[pl.BlockSpec(memory_space=pltpu.VMEM)],
-        out_specs=pl.BlockSpec(memory_space=pltpu.HBM),
-        scratch_shapes=[dma(())],
-        compiler_params=pltpu.CompilerParams(vmem_limit_bytes=4 * 1024 * 1024),
-    )(y)
 
 
 def body(embeddings, *rest):

time: 94.3 us -> 94.3 us (level)
  local copies, waits for them, and re-layouts: 0 us -> 1.32 us
  Pallas kernels: 94.2 us -> 92.9 us
    pallas_call x1 -> x0, Pallas kernels: 1.33 us -> none  [tile_body(): pl.pallas_call(write_kernel, out_shape=jax.ShapeDtypeStruct(y.shape, y.dt...]
    unnamed x0 -> x1, local copies, waits for them, and re-layouts: none -> 1.32 us
where the time goes in v1:
time: 94.3 us; the launch traced here: 94.2 us
  Pallas kernels  92.9 us (99%)
  local copies, waits for them, and re-layouts  1.32 us (1%)
    pallas_call x1, Pallas kernels, tile_body(): pl.pallas_call(functools.partial(tile_kernel, emb_size, dp_size, cores, 1...  92.9 us

profile of v1, /device:TPU:9, one launch (start us, length us, event | category | flops | bytes accessed | tf_op | source)
XLA Modules:
  0.0 94.2 jit_solution(5603042132038808922)
XLA Ops:
  0.0 92.9 %shard_map.64 = bf16[64,64,256]{2,1,0:T(8,128)(2,1)S(1)} custom-call(bf16[64,64,256]{2,1,0:T(8,128)(2,1)} %x_hbm.1, bf16[128,512]{1,0:T(8,128)(2,1)} %w_hbm.1, bf16[32,512]{1,0:T(8,128)(2,1)} %bitcast.1, bf16[32,256]{1,0:T(8,128)(2,1)} %fmb_hbm.1, f32[64,256]{1,0:T(8,128)} %gain_hbm.1, f32[64,256]{1,0:T(8,128)} %bias_hbm.1), custom_call_target="tpu_custom_call" | custom-call | tf_op jit(solution)/shard_map/pallas_call | solution.py:470
  92.9 1.3 %copy.8 = bf16[64,64,256]{2,1,0:T(8,128)(2,1)} copy(bf16[64,64,256]{2,1,0:T(8,128)(2,1)S(1)} %shard_map.64) | data formatting | bytes 4194304

commit v2 on v1

--- a/solution.py
+++ b/solution.py
@@ -269,15 +269,27 @@
     def last_source(receiver):
         return jnp.where(receiver // cores < half, half, half - 1) * cores + cores - 1
 
-    def out_copy(source, peer):
-        return pltpu.make_async_remote_copy(
-            src_ref=done.at[pl.ds(peer * rows, rows)],
-            dst_ref=back.at[source],
+    tail = max(rows // 8, 1)
+    parts = ((0, rows - tail), (rows - tail, tail))
+
+    def out_copy(source, peer, start=0, size=rows, slot=0):
+        return pltpu.make_async_remote_copy(
+            src_ref=done.at[pl.ds(peer * rows + start, size)],
+            dst_ref=back.at[source, pl.ds(start, size)],
             send_sem=send_sem,
-            recv_sem=out_recv.at[(source == last_source(peer)).astype(jnp.int32)],
+            recv_sem=out_recv.at[slot],
             device_id={"emb": peer},
             device_id_type=MESH,
         )
+
+    def send_back(peer):
+        ends = me == last_source(peer)
+        pl.when(jnp.logical_not(ends))(lambda: out_copy(me, peer).start())
+
+        @pl.when(ends)
+        def _():
+            for slot, (start, size) in enumerate(parts, 1):
+                out_copy(me, peer, start, size, slot).start()
 
     def w_copy(i):
         bit = dp_bits[i]
@@ -346,9 +358,9 @@
 
     for source, first in ((proj_hbm, 0), (fmb_hbm, emb_count)):
         target = factors.at[:, pl.ds(first, source.shape[1])]
-        pltpu.make_async_copy(source, target, load_sem.at[2]).start()
+        pltpu.make_async_copy(source, target, load_sem.at[0]).start()
     for i, source in enumerate((gain_hbm, bias_hbm)):
-        pltpu.make_async_copy(source, affine.at[i], load_sem.at[3]).start()
+        pltpu.make_async_copy(source, affine.at[i], load_sem.at[0]).start()
     if chips > 2:
         tell(2)
 
@@ -379,15 +391,14 @@
     def _():
         w_pass(me - core).wait_recv()
 
-    wait_for(factors, load_sem.at[2])
-    wait_for(affine, load_sem.at[3])
+    loaded = 2 * (own.size + factors.size) + 4 * affine.size
+    wait_for(wide.at[0, pl.ds(0, loaded // (4 * LANES))], load_sem.at[0])
 
     def widen(source, taken):
         taken = taken.astype(jnp.float32).reshape(block, width)
         for c in range(len(columns)):
             wide[c, pl.ds(pl.multiple_of(source * block, block), block)] = taken[:, c * LANES:(c + 1) * LANES]
 
-    own_in.wait()
     widen(me, own[...])
     wait_for(got.at[pl.ds(0, others * rows)], in_recv)
 
@@ -430,14 +441,15 @@
                 .astype(jnp.bfloat16)
             )
 
-    def land(source, taken):
-        y_ref[:, pl.ds(pl.multiple_of(source * share, share), share), :] = (
-            taken.astype(jnp.float32) * affine[0][:, None, :] + affine[1][:, None, :]
+    def land(source, taken, start=0):
+        part = pl.ds(start, taken.shape[0])
+        y_ref[part, pl.ds(pl.multiple_of(source * share, share), share), :] = (
+            taken.astype(jnp.float32) * affine[0, part][:, None, :] + affine[1, part][:, None, :]
         ).astype(jnp.bfloat16)
 
     pl.loop(0, emb_size)(narrow)
     land(me, done[pl.ds(me * rows, rows)])
-    same_side_then_across(lambda peer: out_copy(me, peer).start())
+    same_side_then_across(send_back)
 
     @pl.when(core == 0)
     def _():
@@ -454,8 +466,9 @@
         def _():
             land(source, back[source])
 
-    wait_for(back.at[0], out_recv.at[1])
-    land(last, back[last])
+    for slot, (start, size) in enumerate(parts, 1):
+        wait_for(back.at[0, pl.ds(start, size)], out_recv.at[slot])
+        land(last, back[last, pl.ds(start, size)], start)
     wait_for(wide.at[:, pl.ds(0, others * block)], send_sem)
 
 
@@ -487,8 +500,8 @@
             dma((dp_size.bit_length() - 1,)),
             dma(()),
             dma(()),
+            dma((3,)),
             dma((2,)),
-            dma((4,)),
             pltpu.SemaphoreType.REGULAR,
             pltpu.SemaphoreType.REGULAR,
             pltpu.SemaphoreType.REGULAR((max(emb_size // cores - 2, 1),)),

time: 94.3 us -> 94.2 us (level)
  no operation moved by 1% of the time
where the time goes in v2:
time: 94.2 us; the launch traced here: 94.1 us
  Pallas kernels  92.7 us (98%)
  local copies, waits for them, and re-layouts  1.32 us (1%)
    pallas_call x1, Pallas kernels, tile_body(): pl.pallas_call(functools.partial(tile_kernel, emb_size, dp_size, cores, 1...  92.7 us

profile of v2, /device:TPU:9, one launch (start us, length us, event | category | flops | bytes accessed | tf_op | source)
XLA Modules:
  0.0 94.1 jit_solution(12658944959841170386)
XLA Ops:
  0.0 92.7 %shard_map.64 = bf16[64,64,256]{2,1,0:T(8,128)(2,1)S(1)} custom-call(bf16[64,64,256]{2,1,0:T(8,128)(2,1)} %x_hbm.1, bf16[128,512]{1,0:T(8,128)(2,1)} %w_hbm.1, bf16[32,512]{1,0:T(8,128)(2,1)} %bitcast.1, bf16[32,256]{1,0:T(8,128)(2,1)} %fmb_hbm.1, f32[64,256]{1,0:T(8,128)} %gain_hbm.1, f32[64,256]{1,0:T(8,128)} %bias_hbm.1), custom_call_target="tpu_custom_call" | custom-call | tf_op jit(solution)/shard_map/pallas_call | solution.py:483
  92.8 1.3 %copy.8 = bf16[64,64,256]{2,1,0:T(8,128)(2,1)} copy(bf16[64,64,256]{2,1,0:T(8,128)(2,1)S(1)} %shard_map.64) | data formatting | bytes 4194304

commit v3 on v2

--- a/solution.py
+++ b/solution.py
@@ -269,7 +269,7 @@
     def last_source(receiver):
         return jnp.where(receiver // cores < half, half, half - 1) * cores + cores - 1
 
-    tail = max(rows // 8, 1)
+    tail = max(rows // 16, 1)
     parts = ((0, rows - tail), (rows - tail, tail))
 
     def out_copy(source, peer, start=0, size=rows, slot=0):

time: 94.2 us -> 94.2 us (level)
  no operation moved by 1% of the time
where the time goes in v3:
time: 94.2 us; the launch traced here: 94.1 us
  Pallas kernels  92.7 us (98%)
  local copies, waits for them, and re-layouts  1.32 us (1%)
    pallas_call x1, Pallas kernels, tile_body(): pl.pallas_call(functools.partial(tile_kernel, emb_size, dp_size, cores, 1...  92.7 us

profile of v3, /device:TPU:9, one launch (start us, length us, event | category | flops | bytes accessed | tf_op | source)
XLA Modules:
  0.0 94.1 jit_solution(10098415974825182985)
XLA Ops:
  0.0 92.7 %shard_map.64 = bf16[64,64,256]{2,1,0:T(8,128)(2,1)S(1)} custom-call(bf16[64,64,256]{2,1,0:T(8,128)(2,1)} %x_hbm.1, bf16[128,512]{1,0:T(8,128)(2,1)} %w_hbm.1, bf16[32,512]{1,0:T(8,128)(2,1)} %bitcast.1, bf16[32,256]{1,0:T(8,128)(2,1)} %fmb_hbm.1, f32[64,256]{1,0:T(8,128)} %gain_hbm.1, f32[64,256]{1,0:T(8,128)} %bias_hbm.1), custom_call_target="tpu_custom_call" | custom-call | tf_op jit(solution)/shard_map/pallas_call | solution.py:483
  92.7 1.3 %copy.8 = bf16[64,64,256]{2,1,0:T(8,128)(2,1)} copy(bf16[64,64,256]{2,1,0:T(8,128)(2,1)S(1)} %shard_map.64) | data formatting | bytes 4194304
